TPU v7x, 256 devices: a 2x2x32 block of a 4x8x32 slice. The times are simulated.
256 devices in a mesh: group: 4 (over y, x), blk: 64 (over z, core).
Axes of the slice: x: 2, y: 2, z: 32, core: 2. Of those that a mesh axis runs over, the one named last changes fastest.
The devices are a block of a 4x8x32 slice.
Arguments:
- queries: bfloat16 [8, 256, 2048], P('group', 'blk'), parts along dimension 0, may hold values from -160 to 160
- keys: bfloat16 [8, 81920, 256], P('group', 'blk'), parts along dimension 0, may hold values from -4 to 4
- values: bfloat16 [8, 81920, 256], P('group', 'blk'), parts along dimension 0, may hold values from -6 to 6
- lengths: int32 [8], P('group'), parts along dimension 0, may hold values from 61440 to 81920
- offsets: int32 [8], P('group'), parts along dimension 0, may hold values from 51200 to 81664
Outputs:
- attended: bfloat16 [8, 256, 2048], P('group', 'blk'), parts along dimension 0
There are 4 independent parts, one for each index of `group`. A program takes and returns all parts, laid end to end along the dimension named above; each array names one. Nothing has to cross between parts.
All inputs are finite; a program needn't handle non-finite values.
Results may differ from a plain program's by a relative error of at most 0.0085.
Values may be sent and summed in bfloat16 or wider, within the bound.
A program may use at most 64 MiB of HBM per device.

v0:
```python
import math
import jax
import jax.numpy as jnp
from jax import lax
from jax.sharding import PartitionSpec as P

KV_HEADS = 2
HEAD_DIM = 128
masked_low = -1e30


def shard_partial(query_rows, key_rows, value_rows, query_pos, key_pos, lengths):
    micro_count, rows_count, row_width = query_rows.shape
    heads_count = row_width // HEAD_DIM
    group_size = heads_count // KV_HEADS
    query_split = query_rows.reshape(micro_count, rows_count, KV_HEADS, group_size, HEAD_DIM)
    key_split = key_rows.reshape(micro_count, key_rows.shape[1], KV_HEADS, HEAD_DIM)
    value_split = value_rows.reshape(micro_count, value_rows.shape[1], KV_HEADS, HEAD_DIM)
    scores = jnp.einsum(
        "brkgd,bskd->bkgrs", query_split, key_split, preferred_element_type=jnp.float32
    )
    scores = scores * (1.0 / math.sqrt(HEAD_DIM))
    visible = (key_pos[None, None, :] <= query_pos[:, :, None]) & (
        key_pos[None, None, :] < lengths[:, None, None]
    )
    visible = visible[:, None, None, :, :]
    any_visible = jnp.any(visible, axis=-1)
    row_max = jnp.max(jnp.where(visible, scores, masked_low), axis=-1)
    safe_max = jnp.where(any_visible, row_max, 0.0)
    shifted = jnp.where(visible, scores - safe_max[..., None], 0.0)
    weights = jnp.where(visible, jnp.exp(shifted), 0.0)
    totals = jnp.sum(weights, axis=-1)
    bounded = jnp.maximum(totals, 1.0)
    numerator = jnp.einsum(
        "bkgrs,bskd->bkgrd",
        weights.astype(jnp.bfloat16),
        value_split,
        preferred_element_type=jnp.float32,
    )
    partial_value = (numerator / bounded[..., None]).astype(jnp.bfloat16)
    partial_value = jnp.transpose(partial_value, (0, 3, 1, 2, 4)).reshape(
        micro_count, rows_count, row_width
    )
    logsum = jnp.where(any_visible, safe_max + jnp.log(bounded), masked_low)
    logsum = jnp.transpose(logsum, (0, 3, 1, 2)).reshape(micro_count, rows_count, heads_count)
    return (partial_value, logsum)


def body(queries, keys, values, lengths, offsets):
    micro_count, local_rows, row_width = queries.shape
    local_keys = keys.shape[1]
    heads_count = row_width // HEAD_DIM
    shards = lax.axis_size("blk")
    key_pos = lax.axis_index("blk") * local_keys + jnp.arange(local_keys, dtype=jnp.int32)
    visiting = lax.all_gather(queries, "blk", axis=1, tiled=True)
    rows_count = visiting.shape[1]
    block_rows = math.gcd(rows_count, 64)
    block_count = rows_count // block_rows

    def one_block(block_index):
        block_start = block_index * block_rows
        selected = lax.dynamic_slice_in_dim(visiting, block_start, block_rows, 1)
        query_pos = (
            offsets[:, None] + block_start + jnp.arange(block_rows, dtype=jnp.int32)[None, :]
        )
        return shard_partial(selected, keys, values, query_pos, key_pos, lengths)

    block_parts, block_logs = lax.map(one_block, jnp.arange(block_count, dtype=jnp.int32))
    block_parts = jnp.moveaxis(block_parts, 0, 1).reshape(micro_count, rows_count, row_width)
    block_logs = jnp.moveaxis(block_logs, 0, 1).reshape(micro_count, rows_count, heads_count)
    partials = block_parts
    logsums = block_logs
    partials, logsums = (partials, logsums)
    shaped_parts = partials.reshape(micro_count, shards, local_rows, row_width)
    shaped_logs = logsums.reshape(micro_count, shards, local_rows, heads_count)
    home_parts = lax.all_to_all(shaped_parts, "blk", split_axis=1, concat_axis=1, tiled=True)
    home_logs = lax.all_to_all(shaped_logs, "blk", split_axis=1, concat_axis=1, tiled=True)
    row_peak = jnp.max(home_logs, axis=1, keepdims=True)
    scales = jnp.exp(home_logs - row_peak)
    denominator = jnp.sum(scales, axis=1)
    split_parts = home_parts.reshape(micro_count, shards, local_rows, heads_count, HEAD_DIM)
    weighted = jnp.sum(split_parts * scales[..., None], axis=1)
    merged = weighted / denominator[..., None]
    attended = merged.reshape(micro_count, local_rows, row_width).astype(jnp.bfloat16)
    return attended


def solution(mesh):
    return jax.shard_map(
        body,
        mesh=mesh,
        in_specs=(
            P("group", "blk", None),
            P("group", "blk", None),
            P("group", "blk", None),
            P("group"),
            P("group"),
        ),
        out_specs=P("group", "blk", None),
        check_vma=False,
    )
```

profile of v0, /device:TPU:37, one launch (start us, length us, event | category | flops | bytes accessed | tf_op | source)
XLA Modules:
  0.0 481.0 jit_solution(16185152529671269494)
XLA Ops:
  6.6 1.4 copy.51
  8.1 3.8 reshape.97
  11.9 2.9 reshape.98
  14.9 139.4 %all-gather.2.cloned.1.call-done = bf16[2,256,2048]{2,0,1:T(2,128)(2,1)} async-done(((bf16[2,4,2048]{2,0,1:T(2,128)(2,1)}), bf16[2,256,2048]{2,0,1:T(2,128)(2,1)}) %all-gather.2.cloned.1.call-update) | async-done | bytes 2097168 | tf_op jit(solution)/shard_map/all_gather | solution.py:55
  154.3 71.4 %while.14 = (s32[]{:T(128)}, bf16[4,2,64,2048]{3,2,1,0:T(8,128)(2,1)}, f32[4,2,64,16]{2,3,1,0:T(8,128)S(1)}, s32[4]{0:T(128)S(1)}, s32[2]{0:T(128)S(1)}, /*index...) while((s32[]{:T(128)}, ...), condition=%wide.wide.region_4.5_spmd.clone, body=%wide.wide.region_0.4_spmd.clone.sunk | while | flops 1377611520 | bytes 88389816 | solution.py:68
  154.3 0.6 dynamic_slice.15
  155.5 1.4 constant_dynamic-slice_fusion.3
  156.9 0.3 reshape.103
  157.5 0.2 compare_and_fusion.3
  157.6 3.0 fusion.38
  160.6 0.3 and_reduce_fusion.3
  161.0 4.3 fusion.39
  165.3 0.1 fusion.40
  165.5 5.4 %divide_convert_fusion.4 = bf16[2,64,2,8,128]{4,3,1,2,0:T(8,128)(2,1)S(1)} fusion(bf16[2,1280,2,128,1]{3,2,1,0,4:T(2,128)(2,1)S(1)} %bitcast.95, f32[2,2,64,8,1280]{4,3,2,1,0:T(8,128)} %copy-done, f32[2,2,8,64]{2,3,1,0:T(8,128)S(1)} %broadcast_select_fusion.3, pred[2,64,1280]{2,1,0:T(8,128)(4,1)S(1)} %compare_and_fusion.3, ...), kind=kOutput, calls=%fused_computation.15.clone.clone.1 | convolution fusion | flops 684720128 | bytes 12500992 | tf_op jit(solution)/shard_map/while/body/eval_jaxpr/bkgrs,bskd->bkgrd/dot_general | solution.py:34
  171.1 0.2 broadcast_in_dim.143
  171.3 0.9 constant_dynamic-update-slice_fusion.3
  172.1 0.6 dynamic_slice.15
  173.4 1.4 constant_dynamic-slice_fusion.3
  174.8 0.3 reshape.103
  175.3 0.2 compare_and_fusion.3
  175.5 3.0 fusion.38
  178.5 0.3 and_reduce_fusion.3
  178.8 4.3 fusion.39
  183.1 0.1 fusion.40
  183.4 5.4 %divide_convert_fusion.4 = bf16[2,64,2,8,128]{4,3,1,2,0:T(8,128)(2,1)S(1)} fusion(bf16[2,1280,2,128,1]{3,2,1,0,4:T(2,128)(2,1)S(1)} %bitcast.95, f32[2,2,64,8,1280]{4,3,2,1,0:T(8,128)} %copy-done, f32[2,2,8,64]{2,3,1,0:T(8,128)S(1)} %broadcast_select_fusion.3, pred[2,64,1280]{2,1,0:T(8,128)(4,1)S(1)} %compare_and_fusion.3, ...), kind=kOutput, calls=%fused_computation.15.clone.clone.1 | convolution fusion | flops 684720128 | bytes 12500992 | tf_op jit(solution)/shard_map/while/body/eval_jaxpr/bkgrs,bskd->bkgrd/dot_general | solution.py:34
  188.9 0.2 broadcast_in_dim.143
  189.1 0.9 constant_dynamic-update-slice_fusion.3
  190.0 0.6 dynamic_slice.15
  191.3 1.4 constant_dynamic-slice_fusion.3
  192.7 0.3 reshape.103
  193.2 0.2 compare_and_fusion.3
  193.4 3.0 fusion.38
  196.3 0.3 and_reduce_fusion.3
  196.7 4.3 fusion.39
  201.0 0.1 fusion.40
  201.3 5.4 %divide_convert_fusion.4 = bf16[2,64,2,8,128]{4,3,1,2,0:T(8,128)(2,1)S(1)} fusion(bf16[2,1280,2,128,1]{3,2,1,0,4:T(2,128)(2,1)S(1)} %bitcast.95, f32[2,2,64,8,1280]{4,3,2,1,0:T(8,128)} %copy-done, f32[2,2,8,64]{2,3,1,0:T(8,128)S(1)} %broadcast_select_fusion.3, pred[2,64,1280]{2,1,0:T(8,128)(4,1)S(1)} %compare_and_fusion.3, ...), kind=kOutput, calls=%fused_computation.15.clone.clone.1 | convolution fusion | flops 684720128 | bytes 12500992 | tf_op jit(solution)/shard_map/while/body/eval_jaxpr/bkgrs,bskd->bkgrd/dot_general | solution.py:34
  206.8 0.2 broadcast_in_dim.143
  207.0 0.8 constant_dynamic-update-slice_fusion.3
  207.8 0.6 dynamic_slice.15
  209.1 1.4 constant_dynamic-slice_fusion.3
  210.5 0.3 reshape.103
  211.0 0.2 compare_and_fusion.3
  211.2 3.0 fusion.38
  214.2 0.3 and_reduce_fusion.3
  214.5 4.3 fusion.39
  219.1 5.4 %divide_convert_fusion.4 = bf16[2,64,2,8,128]{4,3,1,2,0:T(8,128)(2,1)S(1)} fusion(bf16[2,1280,2,128,1]{3,2,1,0,4:T(2,128)(2,1)S(1)} %bitcast.95, f32[2,2,64,8,1280]{4,3,2,1,0:T(8,128)} %copy-done, f32[2,2,8,64]{2,3,1,0:T(8,128)S(1)} %broadcast_select_fusion.3, pred[2,64,1280]{2,1,0:T(8,128)(4,1)S(1)} %compare_and_fusion.3, ...), kind=kOutput, calls=%fused_computation.15.clone.clone.1 | convolution fusion | flops 684720128 | bytes 12500992 | tf_op jit(solution)/shard_map/while/body/eval_jaxpr/bkgrs,bskd->bkgrd/dot_general | solution.py:34
  224.6 0.2 broadcast_in_dim.143
  224.8 0.8 constant_dynamic-update-slice_fusion.3
  225.7 0.1 copy.54
  225.9 0.8 reshape.95
  226.7 13.8 %all-to-all-start.1 = ((f32[64,1,128]{2,1,0:T(1,128)}), f32[64,1,128]{2,1,0:T(1,128)S(1)}, u32[]{:S(2)}, u32[]{:S(2)}) async-start(f32[64,1,128]{2,1,0:T(1,128)} %reshape.95), calls=%async_computation.1 | async-start | bytes 65536 | tf_op jit(solution)/shard_map/all_to_all | solution.py:77
  240.5 5.1 %copy.53 = bf16[2,4,64,2048]{3,0,2,1:T(2,128)(2,1)} copy(bf16[2,4,64,2048]{3,2,0,1:T(8,128)(2,1)} %bitcast.94) | data formatting | bytes 4194304 | tf_op jit(solution)/shard_map/transpose | solution.py:69
  245.6 16.6 %all-to-all-done.1 = f32[64,1,128]{2,1,0:T(1,128)S(1)} async-done(((f32[64,1,128]{2,1,0:T(1,128)}), f32[64,1,128]{2,1,0:T(1,128)S(1)}, u32[]{:S(2)}, u32[]{:S(2)}) %all-to-all-start.1) | async-done | bytes 32800 | tf_op jit(solution)/shard_map/all_to_all | solution.py:77
  262.2 6.6 %all-to-all-start = ((bf16[2,64,4,2048]{3,0,2,1:T(2,128)(2,1)}), bf16[2,64,4,2048]{3,0,2,1:T(2,128)(2,1)S(1)}, u32[]{:S(2)}, u32[]{:S(2)}) async-start(bf16[2,64,4,2048]{3,0,2,1:T(2,128)(2,1)} %bitcast.93), calls=%async_computation | async-start | bytes 4194304 | tf_op jit(solution)/shard_map/all_to_all | solution.py:76
  268.8 0.5 broadcast.111
  269.4 0.7 reduce.2
  270.1 0.2 reshape.96
  270.4 0.1 fusion.25
  270.5 0.1 copy.56
  270.7 2.6 mul.27
  273.3 5.8 %mul.28 = f32[2,64,4,2048]{3,0,2,1:T(2,128)} reshape(f32[2,64,4,16,128]{4,3,0,2,1:T(8,128)} %mul.27) | data formatting | bytes 8388608 | tf_op jit(solution)/shard_map/mul | solution.py:82
  279.2 189.7 %all-to-all-done = bf16[2,64,4,2048]{3,0,2,1:T(2,128)(2,1)S(1)} async-done(((bf16[2,64,4,2048]{3,0,2,1:T(2,128)(2,1)}), bf16[2,64,4,2048]{3,0,2,1:T(2,128)(2,1)S(1)}, u32[]{:S(2)}, u32[]{:S(2)}) %all-to-all-start) | async-done | bytes 2097184 | tf_op jit(solution)/shard_map/all_to_all | solution.py:76
  468.9 4.5 multiply_reduce_fusion
  473.5 0.6 copy.58
  (68 shorter events, 2.3 us)
Async XLA Ops:
  6.5 147.7 %copy-start.2 = (s32[2]{0:T(128)S(1)}, s32[2]{0:T(128)}, u32[]{:S(2)}) copy-start(s32[2]{0:T(128)} %param.10) | copy-start | bytes 28
  6.5 147.7 %copy-start.3 = (s32[2]{0:T(128)S(1)}, s32[2]{0:T(128)}, u32[]{:S(2)}) copy-start(s32[2]{0:T(128)} %param.11) | copy-start | bytes 28
  6.6 147.7 %all-gather.2.cloned.1.call-start = ((), (), s32[]{:S(2)}) async-start(), calls=%async_computation.2 | async-start | bytes 2129920 | tf_op jit(solution)/shard_map/all_gather | solution.py:55
  160.6 4.7 copy-start
  161.0 4.5 copy-start.1
  178.5 4.7 copy-start
  178.8 4.5 copy-start.1
  196.3 4.7 copy-start
  196.7 4.5 copy-start.1
  214.2 4.7 copy-start
  214.5 4.5 copy-start.1
  226.7 35.6 %all-to-all-start.1 = ((f32[64,1,128]{2,1,0:T(1,128)}), f32[64,1,128]{2,1,0:T(1,128)S(1)}, u32[]{:S(2)}, u32[]{:S(2)}) async-start(f32[64,1,128]{2,1,0:T(1,128)} %reshape.95), calls=%async_computation.1 | async-start | bytes 65536 | tf_op jit(solution)/shard_map/all_to_all | solution.py:77
  262.2 206.7 %all-to-all-start = ((bf16[2,64,4,2048]{3,0,2,1:T(2,128)(2,1)}), bf16[2,64,4,2048]{3,0,2,1:T(2,128)(2,1)S(1)}, u32[]{:S(2)}, u32[]{:S(2)}) async-start(bf16[2,64,4,2048]{3,0,2,1:T(2,128)(2,1)} %bitcast.93), calls=%async_computation | async-start | bytes 4194304 | tf_op jit(solution)/shard_map/all_to_all | solution.py:76
Sparse Core Ops, SparseCore 0:
  9.2 145.0 all-gather.1
where the time goes:
time: 482 us; the launch traced here: 481 us
  waiting for transfers between devices  346 us (72%)
  local copies, waits for them, and re-layouts  38.7 us (8%)
  matrix products  33.6 us (7%)
  other arithmetic  26 us (5%)
  starting transfers between devices  20.4 us (4%)
  between operations  13.5 us (3%)
    all_to_all x1, waiting for transfers between devices, body(): lax.all_to_all(shaped_parts, 'blk', split_axis=1, concat_axis=1, tiled=True)  190 us
    all_gather x1, waiting for transfers between devices, body(): visiting = lax.all_gather(queries, 'blk', axis=1, tiled=True)  139 us
    dot_general x4, matrix products, shard_partial(): jnp.einsum('bkgrs,bskd->bkgrd', weights.astype(jnp.bfloat16), value_split...  21.7 us
    reduce_sum x4, other arithmetic, shard_partial(): totals = jnp.sum(weights, axis=-1)  17.2 us
    all_to_all x1, waiting for transfers between devices, body(): lax.all_to_all(shaped_logs, 'blk', split_axis=1, concat_axis=1, tiled=True)  16.6 us
    all_to_all x1, starting transfers between devices, body(): lax.all_to_all(shaped_logs, 'blk', split_axis=1, concat_axis=1, tiled=True)  13.8 us
    dot_general x4, matrix products, shard_partial(): jnp.einsum('brkgd,bskd->bkgrs', query_split, key_split, preferred_element...  11.8 us
  transfers between devices with their start and end apart: 3, of which 3 were waited for; matrix products, arithmetic and copies ran while one was open for 5% of the time, Pallas kernels for 0%

commit v1 on v0

--- a/solution.py
+++ b/solution.py
@@ -52,7 +52,8 @@
     heads_count = row_width // HEAD_DIM
     shards = lax.axis_size("blk")
     key_pos = lax.axis_index("blk") * local_keys + jnp.arange(local_keys, dtype=jnp.int32)
-    visiting = lax.all_gather(queries, "blk", axis=1, tiled=True)
+    sent = jnp.stack([queries] * lax.axis_size("blk"))
+    visiting = jnp.concatenate(lax.all_to_all(sent, "blk", 0, 0), axis=1)
     rows_count = visiting.shape[1]
     block_rows = math.gcd(rows_count, 64)
     block_count = rows_count // block_rows

time: 482 us -> 553 us (1.15)
  waiting for transfers between devices: 346 us -> 398 us
  starting transfers between devices: 20.4 us -> 48.2 us
  between operations: 13.5 us -> 0.15 us
    all_to_all x0 -> x1, waiting for transfers between devices: none -> 193 us  [body(): visiting = jnp.concatenate(lax.all_to_all(sent, 'blk', 0, 0), axis=1)]
    all_gather x1 -> x0, waiting for transfers between devices: 139 us -> none  [body(): visiting = lax.all_gather(queries, 'blk', axis=1, tiled=True)]
    all_to_all x0 -> x1, starting transfers between devices: none -> 34.4 us  [body(): visiting = jnp.concatenate(lax.all_to_all(sent, 'blk', 0, 0), axis=1)]
    all_to_all x1, starting transfers between devices: 13.8 us -> 7.8 us  [body(): lax.all_to_all(shaped_logs, 'blk', split_axis=1, concat_axis=1, tiled=True)]
  transfers between devices with their start and end apart: 3 -> 3, of which waited for: 3 -> 3; matrix products, arithmetic and copies ran while one was open for 5% -> 4% of each run, Pallas kernels for 0% -> 0%
where the time goes in v1:
time: 553 us; the launch traced here: 551 us
  waiting for transfers between devices  398 us (72%)
  starting transfers between devices  48.2 us (9%)
  local copies, waits for them, and re-layouts  41.7 us (8%)
  matrix products  33.5 us (6%)
  other arithmetic  26 us (5%)
    all_to_all x1, waiting for transfers between devices, body(): visiting = jnp.concatenate(lax.all_to_all(sent, 'blk', 0, 0), axis=1)  193 us
    all_to_all x1, waiting for transfers between devices, body(): lax.all_to_all(shaped_parts, 'blk', split_axis=1, concat_axis=1, tiled=True)  187 us
    all_to_all x1, starting transfers between devices, body(): visiting = jnp.concatenate(lax.all_to_all(sent, 'blk', 0, 0), axis=1)  34.4 us
    dot_general x4, matrix products, shard_partial(): jnp.einsum('bkgrs,bskd->bkgrd', weights.astype(jnp.bfloat16), value_split...  21.7 us
    all_to_all x1, waiting for transfers between devices, body(): lax.all_to_all(shaped_logs, 'blk', split_axis=1, concat_axis=1, tiled=True)  17.5 us
    reduce_sum x4, other arithmetic, shard_partial(): totals = jnp.sum(weights, axis=-1)  17.2 us
    dot_general x4, matrix products, shard_partial(): jnp.einsum('brkgd,bskd->bkgrs', query_split, key_split, preferred_element...  11.8 us
  transfers between devices with their start and end apart: 3, of which 3 were waited for; matrix products, arithmetic and copies ran while one was open for 4% of the time, Pallas kernels for 0%

profile of v1, /device:TPU:37, one launch (start us, length us, event | category | flops | bytes accessed | tf_op | source)
XLA Modules:
  0.0 550.8 jit_solution(17782790158396431401)
XLA Ops:
  0.0 3.3 stack.2
  3.3 34.4 %all-to-all-start = ((bf16[64,2,4,2048]{3,2,1,0:T(4,128)(2,1)}), bf16[64,2,4,2048]{3,2,1,0:T(4,128)(2,1)S(1)}, u32[]{:S(2)}, u32[]{:S(2)}) async-start(bf16[64,2,4,2048]{3,2,1,0:T(4,128)(2,1)} %stack.2), calls=%async_computation | async-start | bytes 4194304 | tf_op jit(solution)/shard_map/all_to_all | solution.py:56
  37.7 1.2 reshape.107
  38.9 2.9 reshape.108
  41.9 193.1 %all-to-all-done = bf16[64,2,4,2048]{3,2,1,0:T(4,128)(2,1)S(1)} async-done(((bf16[64,2,4,2048]{3,2,1,0:T(4,128)(2,1)}), bf16[64,2,4,2048]{3,2,1,0:T(4,128)(2,1)S(1)}, u32[]{:S(2)}, u32[]{:S(2)}) %all-to-all-start) | async-done | bytes 2097184 | tf_op jit(solution)/shard_map/all_to_all | solution.py:56
  235.0 3.5 copy.61
  238.4 71.9 %while.14 = (s32[]{:T(128)}, bf16[4,2,64,2048]{3,2,1,0:T(8,128)(2,1)}, f32[4,2,64,16]{2,3,1,0:T(8,128)S(1)}, s32[4]{0:T(128)S(1)}, s32[2]{0:T(128)S(1)}, /*index...) while((s32[]{:T(128)}, ...), condition=%wide.wide.region_4.5_spmd.clone, body=%wide.wide.region_0.4_spmd.clone.sunk | while | flops 1377611520 | bytes 88389816 | solution.py:69
  238.4 0.7 dynamic_slice.15
  239.8 1.4 constant_dynamic-slice_fusion.3
  241.2 0.3 reshape.113
  241.7 0.2 compare_and_fusion.3
  241.9 3.0 fusion.38
  244.9 0.3 and_reduce_fusion.3
  245.3 4.3 fusion.39
  249.6 0.1 fusion.40
  249.8 5.4 divide_convert_fusion.4
  255.3 0.2 broadcast_in_dim.143
  255.6 0.9 constant_dynamic-update-slice_fusion.3
  256.4 0.7 dynamic_slice.15
  257.8 1.4 constant_dynamic-slice_fusion.3
  259.2 0.3 reshape.113
  259.7 0.2 compare_and_fusion.3
  259.9 3.0 fusion.38
  262.9 0.3 and_reduce_fusion.3
  263.2 4.3 fusion.39
  267.8 5.4 divide_convert_fusion.4
  273.3 0.2 broadcast_in_dim.143
  273.5 0.9 constant_dynamic-update-slice_fusion.3
  274.4 0.7 dynamic_slice.15
  275.8 1.4 constant_dynamic-slice_fusion.3
  277.2 0.3 reshape.113
  277.7 0.2 compare_and_fusion.3
  277.9 3.0 fusion.38
  280.9 0.3 and_reduce_fusion.3
  281.2 4.3 fusion.39
  285.8 5.4 divide_convert_fusion.4
  291.3 0.2 broadcast_in_dim.143
  291.5 0.8 constant_dynamic-update-slice_fusion.3
  292.4 0.7 dynamic_slice.15
  293.7 1.4 constant_dynamic-slice_fusion.3
  295.1 0.3 reshape.113
  295.6 0.2 compare_and_fusion.3
  295.8 3.0 fusion.38
  298.8 0.3 and_reduce_fusion.3
  299.2 4.3 fusion.39
  303.7 5.4 divide_convert_fusion.4
  309.2 0.2 broadcast_in_dim.143
  309.5 0.8 constant_dynamic-update-slice_fusion.3
  310.3 0.1 copy.64
  310.5 0.8 reshape.105
  311.3 7.8 %all-to-all-start.2 = ((f32[64,1,128]{2,1,0:T(1,128)}), f32[64,1,128]{2,1,0:T(1,128)S(1)}, u32[]{:S(2)}, u32[]{:S(2)}) async-start(f32[64,1,128]{2,1,0:T(1,128)} %reshape.105), calls=%async_computation.2 | async-start | bytes 65536 | tf_op jit(solution)/shard_map/all_to_all | solution.py:78
  319.1 5.1 copy.63
  324.3 17.5 %all-to-all-done.2 = f32[64,1,128]{2,1,0:T(1,128)S(1)} async-done(((f32[64,1,128]{2,1,0:T(1,128)}), f32[64,1,128]{2,1,0:T(1,128)S(1)}, u32[]{:S(2)}, u32[]{:S(2)}) %all-to-all-start.2) | async-done | bytes 32800 | tf_op jit(solution)/shard_map/all_to_all | solution.py:78
  341.8 6.0 %all-to-all-start.1 = ((bf16[2,64,4,2048]{3,0,2,1:T(2,128)(2,1)}), bf16[2,64,4,2048]{3,0,2,1:T(2,128)(2,1)S(1)}, u32[]{:S(2)}, u32[]{:S(2)}) async-start(bf16[2,64,4,2048]{3,0,2,1:T(2,128)(2,1)} %bitcast.96), calls=%async_computation.1 | async-start | bytes 4194304 | tf_op jit(solution)/shard_map/all_to_all | solution.py:77
  347.9 0.5 broadcast.113
  348.4 0.7 reduce.2
  349.1 0.2 reshape.106
  349.4 0.1 fusion.25
  349.5 0.1 copy.66
  349.7 2.6 mul.27
  352.3 5.8 %mul.28 = f32[2,64,4,2048]{3,0,2,1:T(2,128)} reshape(f32[2,64,4,16,128]{4,3,0,2,1:T(8,128)} %mul.27) | data formatting | bytes 8388608 | tf_op jit(solution)/shard_map/mul | solution.py:83
  358.2 187.4 %all-to-all-done.1 = bf16[2,64,4,2048]{3,0,2,1:T(2,128)(2,1)S(1)} async-done(((bf16[2,64,4,2048]{3,0,2,1:T(2,128)(2,1)}), bf16[2,64,4,2048]{3,0,2,1:T(2,128)(2,1)S(1)}, u32[]{:S(2)}, u32[]{:S(2)}) %all-to-all-start.1) | async-done | bytes 2097184 | tf_op jit(solution)/shard_map/all_to_all | solution.py:77
  545.6 4.5 multiply_reduce_fusion
  550.2 0.6 copy.68
  (70 shorter events, 2.4 us)
Async XLA Ops:
  0.0 37.6 %copy-start.1 = (bf16[2,1280,256]{2,1,0:T(8,128)(2,1)S(1)}, bf16[2,1280,256]{2,1,0:T(8,128)(2,1)}, u32[]{:S(2)}) copy-start(bf16[2,1280,256]{2,1,0:T(8,128)(2,1)} %param.9) | copy-start | bytes 3932164
  3.3 231.7 %all-to-all-start = ((bf16[64,2,4,2048]{3,2,1,0:T(4,128)(2,1)}), bf16[64,2,4,2048]{3,2,1,0:T(4,128)(2,1)S(1)}, u32[]{:S(2)}, u32[]{:S(2)}) async-start(bf16[64,2,4,2048]{3,2,1,0:T(4,128)(2,1)} %stack.2), calls=%async_computation | async-start | bytes 4194304 | tf_op jit(solution)/shard_map/all_to_all | solution.py:56
  37.7 200.8 %copy-start.3 = (s32[2]{0:T(128)S(1)}, s32[2]{0:T(128)}, u32[]{:S(2)}) copy-start(s32[2]{0:T(128)} %param.10) | copy-start | bytes 28
  37.7 200.8 %copy-start.4 = (s32[2]{0:T(128)S(1)}, s32[2]{0:T(128)}, u32[]{:S(2)}) copy-start(s32[2]{0:T(128)} %param.11) | copy-start | bytes 28
  244.9 4.7 copy-start
  245.2 4.5 copy-start.2
  262.9 4.7 copy-start
  263.2 4.5 copy-start.2
  280.9 4.7 copy-start
  281.2 4.5 copy-start.2
  298.8 4.7 copy-start
  299.2 4.5 copy-start.2
  311.3 30.5 %all-to-all-start.2 = ((f32[64,1,128]{2,1,0:T(1,128)}), f32[64,1,128]{2,1,0:T(1,128)S(1)}, u32[]{:S(2)}, u32[]{:S(2)}) async-start(f32[64,1,128]{2,1,0:T(1,128)} %reshape.105), calls=%async_computation.2 | async-start | bytes 65536 | tf_op jit(solution)/shard_map/all_to_all | solution.py:78
  341.8 203.8 %all-to-all-start.1 = ((bf16[2,64,4,2048]{3,0,2,1:T(2,128)(2,1)}), bf16[2,64,4,2048]{3,0,2,1:T(2,128)(2,1)S(1)}, u32[]{:S(2)}, u32[]{:S(2)}) async-start(bf16[2,64,4,2048]{3,0,2,1:T(2,128)(2,1)} %bitcast.96), calls=%async_computation.1 | async-start | bytes 4194304 | tf_op jit(solution)/shard_map/all_to_all | solution.py:77
